TPU v7x, 256 devices: a whole 4x4x8 slice. The times are simulated.
256 devices in a mesh: dp: 8 (over z), expert: 32 (over x, y, core).
Axes of the slice: x: 4, y: 4, z: 8, core: 2. Of those that a mesh axis runs over, the one named last changes fastest.
Arguments:
- tokens: bfloat16 [65536, 2048], P(('dp', 'expert')), may hold values from -6 to 6
- expert_ranks: int32 [32, 65536], P(None, ('dp', 'expert')), may hold values from 0 to 65535, as said below
- capacity: int32 [32], replicated, may hold values from 512 to 1024, as said below
- weight_in: bfloat16 [32, 2048, 8192], P('expert', None, 'dp'), may hold values from -0.125 to 0.125
- weight_out: bfloat16 [32, 8192, 2048], P('expert', 'dp'), may hold values from -0.0625 to 0.0625
- gate_weights: float32 [32, 1024], P('expert', 'dp'), may hold values from 0.05 to 1
Outputs:
- combined: bfloat16 [65536, 2048], P(('dp', 'expert'))
Inputs may be any that keep to these rules, and one draw needn't show every extreme that they name: `expert_ranks`: for each expert the ranks are a permutation of 0 to 65535. Of the 256 tokens of one device, at most 8 have rank under 1024 for one expert; for an expert of capacity 1024, some devices have exactly 8. At least one expert has capacity 1024.
All inputs are finite; a program needn't handle non-finite values.
Results may differ from a plain program's by a relative error of at most 0.0053.
Values may be sent and summed in bfloat16 or wider, within the bound.
No kernel may reach another device: no remote copies, remote signals or barrier semaphores. Data moves between devices by JAX's collectives and lax.ppermute only.
A program may use at most 64 MiB of HBM per device.

v0:
```python
import jax
import jax.numpy as jnp
from jax import lax
from jax.sharding import Mesh
from jax.sharding import PartitionSpec as P

MOST = 8
LANES = 128
EXPERT = ("expert_0", "expert_1", "expert_2")
DP_EXPERT = ("dp", "expert_0", "expert_1", "expert_2")


def exclusive(values):
    return jnp.cumsum(values) - values


def on_device(tokens, expert_ranks, capacity, weight_in, weight_out, gate_weights):
    dp_count = lax.axis_size("dp")
    expert_count = lax.axis_size(EXPERT)
    token_count, width = tokens.shape
    slots_dp = gate_weights.shape[1]
    rows_all = expert_count * MOST
    own_dp = lax.axis_index("dp")
    own_expert = lax.axis_index(EXPERT)
    chosen = expert_ranks < capacity[:, None]
    chosen_int = chosen.astype(jnp.int32)
    counts = jnp.sum(chosen_int, axis=1)
    before = jnp.cumsum(chosen_int, axis=1) - chosen_int
    places = lax.broadcasted_iota(jnp.int32, (expert_count, MOST, token_count), 1)
    pack_table = jnp.logical_and(chosen[:, None, :], before[:, None, :] == places)
    pack_table = pack_table.astype(jnp.bfloat16).reshape(rows_all, token_count)
    packed = jnp.dot(pack_table, tokens, preferred_element_type=jnp.float32).astype(jnp.bfloat16)
    arrived_rows = lax.all_to_all(
        packed.reshape(expert_count, MOST, width), EXPERT, split_axis=0, concat_axis=0, tiled=True
    ).reshape(rows_all, width)
    device_ids = lax.broadcasted_iota(jnp.int32, (expert_count, expert_count), 0)
    expert_ids = lax.broadcasted_iota(jnp.int32, (expert_count, expert_count), 1)
    table = jnp.where(device_ids == own_expert, counts[None, :], 0)
    table = lax.psum(table.reshape(-1, LANES), EXPERT).reshape(expert_count, expert_count)
    arrived = jnp.sum(jnp.where(expert_ids == own_expert, table, 0), axis=1)
    plane_ids = lax.broadcasted_iota(jnp.int32, (dp_count, LANES), 0)
    lane_ids = lax.broadcasted_iota(jnp.int32, (dp_count, LANES), 1)
    plane_row = jnp.pad(jnp.sum(table, axis=0).astype(jnp.float32), (0, LANES - expert_count))
    both = jnp.concatenate(
        [
            jnp.where(plane_ids == own_dp, plane_row[None, :], 0.0),
            jnp.where(plane_ids == own_dp, gate_weights.reshape(-1, LANES), 0.0),
        ]
    )
    both = lax.psum(both, "dp")
    plane_counts = both[:dp_count].astype(jnp.int32)
    most_rows = jnp.max(plane_counts)
    earlier = jnp.logical_and(plane_ids < own_dp, lane_ids == own_expert)
    first_slot = jnp.sum(jnp.where(earlier, plane_counts, 0))
    gates_all = jnp.concatenate([both[dp_count:].reshape(-1), jnp.zeros((rows_all,), jnp.float32)])
    within = lax.broadcasted_iota(jnp.int32, (expert_count, MOST), 1)
    target = jnp.where(within < arrived[:, None], exclusive(arrived)[:, None] + within, -1).reshape(
        rows_all
    )

    def experts(rows, plane_rows):
        slot_ids = lax.broadcasted_iota(jnp.int32, (rows_all, plane_rows), 1)
        place_table = (target[:, None] == slot_ids).astype(jnp.bfloat16)
        plane = lax.dot_general(
            place_table, rows, (((0,), (0,)), ((), ())), preferred_element_type=jnp.float32
        ).astype(jnp.bfloat16)
        slot_rows = lax.all_gather(plane, "dp", axis=0, tiled=True)
        hidden = jnp.maximum(
            jnp.dot(slot_rows, weight_in[0], preferred_element_type=jnp.float32), 0.0
        ).astype(jnp.bfloat16)
        share = jnp.dot(hidden, weight_out[0], preferred_element_type=jnp.float32)
        out = lax.psum_scatter(
            share.astype(jnp.bfloat16), "dp", scatter_dimension=0, tiled=True
        ).astype(jnp.float32)
        gates = lax.dynamic_slice_in_dim(gates_all, first_slot, plane_rows, 0)
        scaled = (gates[:, None] * out).astype(jnp.bfloat16)
        returned = jnp.dot(place_table, scaled, preferred_element_type=jnp.float32)
        return returned.astype(jnp.bfloat16)

    fair = slots_dp + slots_dp // 4
    sent_back = lax.cond(
        most_rows <= fair,
        lambda rows: experts(rows, fair),
        lambda rows: experts(rows, rows_all),
        arrived_rows,
    )
    results = lax.all_to_all(
        sent_back.reshape(expert_count, MOST, width),
        EXPERT,
        split_axis=0,
        concat_axis=0,
        tiled=True,
    ).reshape(rows_all, width)
    combined = lax.dot_general(
        pack_table, results, (((0,), (0,)), ((), ())), preferred_element_type=jnp.float32
    )
    return combined.astype(jnp.bfloat16)


def solution(mesh):
    split = Mesh(
        mesh.devices.reshape(mesh.shape["dp"], 4, 4, 2), ("dp", "expert_0", "expert_1", "expert_2")
    )
    placed = (
        P(DP_EXPERT, None),
        P(None, DP_EXPERT),
        P(),
        P(EXPERT, None, "dp"),
        P(EXPERT, "dp", None),
        P(EXPERT, "dp"),
    )
    return jax.shard_map(
        on_device, mesh=split, in_specs=placed, out_specs=P(DP_EXPERT, None), check_vma=False
    )
```

profile of v0, /device:TPU:1, one launch (start us, length us, event | category | flops | bytes accessed | tf_op | source)
XLA Modules:
  0.0 348.8 jit_solution(17893966849262882347)
XLA Ops:
  6.5 0.9 convert_bitcast_fusion.1
  7.5 0.6 reduce-window.18
  8.1 0.2 slice_reduce_fusion
  8.3 0.1 iota.90
  8.4 0.1 convert_subtract_fusion
  8.5 1.5 fusion.19
  10.0 8.6 %all-to-all-start = ((bf16[32,8,2048]{2,1,0:T(8,128)(2,1)}), bf16[32,8,2048]{2,1,0:T(8,128)(2,1)S(1)}, u32[]{:S(2)}, u32[]{:S(2)}) async-start(bf16[32,8,2048]{2,1,0:T(8,128)(2,1)} %fusion.19), calls=%async_computation.2 | async-start | bytes 2097152 | tf_op jit(solution)/shard_map/all_to_all | solution.py:33
  18.7 0.1 iota.80
  18.9 127.0 %psum.14 = s32[32,32]{1,0:T(8,128)S(1)} all-reduce(s32[32,32]{1,0:T(8,128)S(1)} %reshape.73), channel_id=1, replica_groups=mesh['dp'=8,'expert_0'=4,'expert_1'=4,'expert_2'=2] {'expert_0','expert_..., use_global_device_ids=true, to_apply=%region_3.4 | all-reduce | flops 1024 | bytes 8192 | tf_op jit(solution)/shard_map/psum | solution.py:39
  145.9 0.1 select_reduce_fusion
  146.1 16.5 %psum.15 = f32[16,128]{1,0:T(8,128)S(1)} all-reduce(f32[16,128]{1,0:T(8,128)S(1)} %pad_maximum_fusion), channel_id=1, replica_groups=mesh['dp'=8,'expert_0'=4,'expert_1'=4,'expert_2'=2] {'dp'}, use_global_device_ids=true, to_apply=%region_5.6 | all-reduce | flops 2048 | bytes 16384 | tf_op jit(solution)/shard_map/psum | solution.py:50
  162.7 0.8 select_reduce_fusion.1
  164.2 0.1 copy.19
  164.3 0.1 reduce.1
  164.5 151.7 %conditional.2 = (bf16[256,2048]{1,0:T(8,128)(2,1)S(1)}) conditional(s32[]{:T(128)} %convert_element_type.61, (s32[32,8]{1,0:T(8,128)S(1)}, s32[]{:T(128)}, f32[1280]{0:T(1024)S(1)}, bf16[256,2048]{1,0:T(8,128)(2,1)S(1)}, bf16[1,2048,1024]{2,1,0:T(8,128)(2,1)}, /*index=5*/bf16[1,1024,2048]{2,1,0:T(8,128)(2,1)}) %tuple.30, (s32[32,8]{1,0:T(8,128)S(1)}, ...), branch_computations={%region_10.12_spmd, %region_12.14_spmd} | conditional | flops 17727356928 | bytes 85990520
  164.6 0.1 eq.49
  164.7 1.3 convolution_convert_fusion.3
  166.0 0.2 reduce-scatter.5.cloned.1.call-start
  166.2 67.1 %all-gather.5.cloned.1.call-done = bf16[1280,2048]{1,0:T(8,128)(2,1)} async-done(((bf16[160,2048]{1,0:T(8,128)(2,1)}), bf16[1280,2048]{1,0:T(8,128)(2,1)}) %all-gather.5.cloned.1.call-update) | async-done | bytes 5242896 | tf_op jit(solution)/shard_map/cond/branch_1_fun/all_gather | solution.py:67
  233.4 16.9 %convolution_convert_fusion.2 = bf16[1280,2048]{1,0:T(8,128)(2,1)} fusion(bf16[1,1024,2048]{2,1,0:T(8,128)(2,1)} %get-tuple-element.45, bf16[1280,2048]{1,0:T(8,128)(2,1)} %all-gather.5.cloned.1.call-done, bf16[1,2048,1024]{2,1,0:T(8,128)(2,1)} %get-tuple-element.44), kind=kOutput, calls=%fused_computation.13 | convolution fusion | flops 10742661120 | bytes 18874368 | tf_op jit(solution)/shard_map/cond/branch_1_fun/dot_general | solution.py:71
  252.0 62.3 %reduce-scatter.5.cloned.1.call-done = bf16[160,2048]{1,0:T(8,128)(2,1)} async-done(((bf16[1280,2048]{1,0:T(8,128)(2,1)}), bf16[160,2048]{1,0:T(8,128)(2,1)}) %reduce-scatter.5.cloned.1.call-update) | async-done | bytes 655376 | tf_op jit(solution)/shard_map/cond/branch_1_fun/reduce_scatter | solution.py:72
  314.4 1.6 fusion.13
  316.2 24.3 %all_to_all.10 = bf16[32,8,2048]{2,1,0:T(8,128)(2,1)S(1)} all-to-all(bf16[32,8,2048]{2,1,0:T(8,128)(2,1)S(1)} %bitcast.57), channel_id=1, replica_groups=mesh['dp'=8,'expert_0'=4,'expert_1'=4,'expert_2'=2] {'expert_0','expert_..., dimensions={0} | all-to-all | bytes 2097152 | tf_op jit(solution)/shard_map/all_to_all | solution.py:87
  340.5 1.5 fusion.18
  (32 shorter events, 0.7 us)
Async XLA Ops:
  6.5 2.0 copy-start
  6.5 139.5 %copy-start.1 = (f32[1,128]{1,0:T(1,128)S(1)}, f32[1,128]{1,0:T(1,128)}, u32[]{:S(2)}) copy-start(f32[1,128]{1,0:T(1,128)} %param.13) | copy-start | bytes 1540
  10.0 154.5 %all-to-all-start = ((bf16[32,8,2048]{2,1,0:T(8,128)(2,1)}), bf16[32,8,2048]{2,1,0:T(8,128)(2,1)S(1)}, u32[]{:S(2)}, u32[]{:S(2)}) async-start(bf16[32,8,2048]{2,1,0:T(8,128)(2,1)} %fusion.19), calls=%async_computation.2 | async-start | bytes 2097152 | tf_op jit(solution)/shard_map/all_to_all | solution.py:33
  164.5 68.8 %all-gather.5.cloned.1.call-start = ((), (), s32[]{:S(2)}) async-start(), calls=%async_computation.6 | async-start | bytes 5898240 | tf_op jit(solution)/shard_map/cond/branch_1_fun/all_gather | solution.py:67
  166.0 148.4 %reduce-scatter.5.cloned.1.call-start = ((), (), s32[]{:S(2)}) async-start(), calls=%async_computation.7 | async-start | bytes 5898240 | tf_op jit(solution)/shard_map/cond/branch_1_fun/reduce_scatter | solution.py:72
Sparse Core Ops, SparseCore 0:
  167.1 66.1 all-gather.4
  250.4 63.9 reduce-scatter.4
where the time goes:
time: 349 us
  blocking collectives  168 us (48%)
  waiting for transfers between devices  129 us (37%)
  matrix products  22.7 us (7%)
  between operations  14.2 us (4%)
  starting transfers between devices  8.84 us (3%)
    psum x1, blocking collectives, on_device(): lax.psum(table.reshape(-1, LANES), EXPERT)  127 us
    all_gather x1, waiting for transfers between devices, experts(): slot_rows = lax.all_gather(plane, 'dp', axis=0, tiled=True)  67.1 us
    reduce_scatter x1, waiting for transfers between devices, experts(): lax.psum_scatter(share.astype(jnp.bfloat16), 'dp', scatter_dimension=0, t...  62.3 us
    all_to_all x1, blocking collectives, on_device(): lax.all_to_all(sent_back.reshape(expert_count, MOST, width), EXPERT, spli...  24.3 us
    dot_general x1, matrix products, experts(): share = jnp.dot(hidden, weight_out[0], preferred_element_type=jnp.float32)  16.9 us
    psum x1, blocking collectives, on_device(): both = lax.psum(both, 'dp')  16.5 us
    all_to_all x1, starting transfers between devices, on_device(): lax.all_to_all(packed.reshape(expert_count, MOST, width), EXPERT, split_a...  8.58 us
  transfers between devices with their start and end apart: 3, of which 2 were waited for; matrix products, arithmetic and copies ran while one was open for 1% of the time, Pallas kernels for 0%

commit v1 on v0

--- a/solution.py
+++ b/solution.py
@@ -8,6 +8,28 @@
 LANES = 128
 EXPERT = ("expert_0", "expert_1", "expert_2")
 DP_EXPERT = ("dp", "expert_0", "expert_1", "expert_2")
+
+
+def in_order(blocks, dim):
+    blocks = jnp.moveaxis(blocks, 0, dim)
+    dims = blocks.shape
+    return blocks.reshape(*dims[:dim], dims[dim] * dims[dim + 1], *dims[dim + 2 :])
+
+
+def gather_around(value, axis, dim):
+    count = lax.axis_size(axis)
+    pairs = [(i, (i + 1) % count) for i in range(count)]
+    back = [(b, a) for a, b in pairs]
+    lower, upper = ([], [])
+    for lap in range(count - 1):
+        if lap % 2 == 0:
+            lower.append(lax.ppermute(lower[-1] if lower else value, axis, pairs))
+        else:
+            upper.append(lax.ppermute(upper[-1] if upper else value, axis, back))
+    blocks = jnp.stack([*lower[::-1], value, *upper])
+    shift = lax.axis_index(axis) - len(lower)
+    blocks = blocks[(jnp.arange(count) - shift) % count]
+    return in_order(blocks, dim)
 
 
 def exclusive(values):
@@ -64,7 +86,7 @@
         plane = lax.dot_general(
             place_table, rows, (((0,), (0,)), ((), ())), preferred_element_type=jnp.float32
         ).astype(jnp.bfloat16)
-        slot_rows = lax.all_gather(plane, "dp", axis=0, tiled=True)
+        slot_rows = gather_around(plane, "dp", 0)
         hidden = jnp.maximum(
             jnp.dot(slot_rows, weight_in[0], preferred_element_type=jnp.float32), 0.0
         ).astype(jnp.bfloat16)

time: 349 us -> 368 us (1.054)
  local copies, waits for them, and re-layouts: 0.89 us -> 17.1 us
  starting transfers between devices: 8.84 us -> 16.8 us
  waiting for transfers between devices: 129 us -> 124 us
    all_gather x1 -> x0, waiting for transfers between devices: 67.1 us -> none  [experts(): slot_rows = lax.all_gather(plane, 'dp', axis=0, tiled=True)]
    ppermute x0 -> x7, waiting for transfers between devices: none -> 54.3 us  [the longest x4 54.3 us: gather_around(): lower.append(lax.ppermute(lower[-1] if lower else value, axis, pairs))]
    another operation x2 -> x10, local copies, waits for them, and re-layouts: 0.09 us -> 10.6 us
    ppermute x0 -> x7, starting transfers between devices: none -> 8.19 us  [the longest x3 8.1 us: gather_around(): upper.append(lax.ppermute(upper[-1] if upper else value, axis, back))]
    reduce_scatter x1, waiting for transfers between devices: 62.3 us -> 69.5 us  [experts(): lax.psum_scatter(share.astype(jnp.bfloat16), 'dp', scatter_dimension=0, t...]
    gather x0 -> x1, local copies, waits for them, and re-layouts: none -> 5.72 us  [gather_around(): blocks = blocks[(jnp.arange(count) - shift) % count]]
  transfers between devices with their start and end apart: 3 -> 9, of which waited for: 2 -> 5; matrix products, arithmetic and copies ran while one was open for 1% -> 3% of each run, Pallas kernels for 0% -> 0%
where the time goes in v1:
time: 368 us; the launch traced here: 367 us
  blocking collectives  168 us (46%)
  waiting for transfers between devices  124 us (34%)
  matrix products  21.9 us (6%)
  local copies, waits for them, and re-layouts  17.1 us (5%)
  starting transfers between devices  16.8 us (5%)
  between operations  14.2 us (4%)
    psum x1, blocking collectives, on_device(): lax.psum(table.reshape(-1, LANES), EXPERT)  127 us
    reduce_scatter x1, waiting for transfers between devices, experts(): lax.psum_scatter(share.astype(jnp.bfloat16), 'dp', scatter_dimension=0, t...  69.5 us
    ppermute x4, waiting for transfers between devices, gather_around(): lower.append(lax.ppermute(lower[-1] if lower else value, axis, pairs))  54.3 us
    all_to_all x1, blocking collectives, on_device(): lax.all_to_all(sent_back.reshape(expert_count, MOST, width), EXPERT, spli...  24.3 us
    dot_general x1, matrix products, experts(): share = jnp.dot(hidden, weight_out[0], preferred_element_type=jnp.float32)  16.9 us
    psum x1, blocking collectives, on_device(): both = lax.psum(both, 'dp')  16.5 us
    another operation x9, local copies, waits for them, and re-layouts  9.64 us
    all_to_all x1, starting transfers between devices, on_device(): lax.all_to_all(packed.reshape(expert_count, MOST, width), EXPERT, split_a...  8.57 us
  transfers between devices with their start and end apart: 9, of which 5 were waited for; matrix products, arithmetic and copies ran while one was open for 3% of the time, Pallas kernels for 0%

profile of v1, /device:TPU:1, one launch (start us, length us, event | category | flops | bytes accessed | tf_op | source)
XLA Modules:
  0.0 367.1 jit_solution(4805389858318638823)
XLA Ops:
  6.5 0.9 convert_bitcast_fusion.1
  8.5 1.5 fusion.23
  10.0 8.6 %all-to-all-start = ((bf16[32,8,2048]{2,1,0:T(8,128)(2,1)}), bf16[32,8,2048]{2,1,0:T(8,128)(2,1)S(1)}, u32[]{:S(2)}, u32[]{:S(2)}) async-start(bf16[32,8,2048]{2,1,0:T(8,128)(2,1)} %fusion.23), calls=%async_computation.2 | async-start | bytes 2097152 | tf_op jit(solution)/shard_map/all_to_all | solution.py:55
  18.9 127.0 %psum.14 = s32[32,32]{1,0:T(8,128)S(1)} all-reduce(s32[32,32]{1,0:T(8,128)S(1)} %reshape.177), channel_id=1, replica_groups=mesh['dp'=8,'expert_0'=4,'expert_1'=4,'expert_2'=2] {'expert_0','expert_..., use_global_device_ids=true, to_apply=%region_3.4 | all-reduce | flops 1024 | bytes 8192 | tf_op jit(solution)/shard_map/psum | solution.py:61
  147.1 16.5 %psum.15 = f32[16,128]{1,0:T(8,128)S(1)} all-reduce(f32[16,128]{1,0:T(8,128)S(1)} %pad_maximum_fusion), channel_id=1, replica_groups=mesh['dp'=8,'expert_0'=4,'expert_1'=4,'expert_2'=2] {'dp'}, use_global_device_ids=true, to_apply=%region_5.6 | all-reduce | flops 2048 | bytes 16384 | tf_op jit(solution)/shard_map/psum | solution.py:72
  165.2 169.3 %conditional.2 = (bf16[256,2048]{1,0:T(8,128)(2,1)S(1)}) conditional(s32[]{:T(128)} %convert_element_type.61, (s32[32,8]{1,0:T(8,128)S(1)}, s32[]{:T(128)}, f32[1280]{0:T(1024)S(1)}, bf16[256,2048]{1,0:T(8,128)(2,1)S(1)}, bf16[1,2048,1024]{2,1,0:T(8,128)(2,1)}, /*index=5*/bf16[1,1024,2048]{2,1,0:T(8,128)(2,1)}) %tuple.26, (s32[32,8]{1,0:T(8,128)S(1)}, ...), branch_computations={%region_10.12_spmd, %region_12.14_spmd} | conditional | flops 17727358976 | bytes 124792344
  166.1 10.7 %collective-permute-done.7 = bf16[160,2048]{1,0:T(8,128)(2,1)S(1)} collective-permute-done((bf16[160,2048]{1,0:T(8,128)(2,1)S(1)}, bf16[160,2048]{1,0:T(8,128)(2,1)S(1)}, u32[]{:S(2)}, u32[]{:S(2)}) %collective-permute-start.7) | collective-permute-done | bytes 655392 | tf_op jit(solution)/shard_map/cond/branch_1_fun/ppermute | solution.py:26
  176.8 2.7 collective-permute-start.11
  179.5 14.2 %collective-permute-done.8 = bf16[160,2048]{1,0:T(8,128)(2,1)S(1)} collective-permute-done((bf16[160,2048]{1,0:T(8,128)(2,1)S(1)}, bf16[160,2048]{1,0:T(8,128)(2,1)S(1)}, u32[]{:S(2)}, u32[]{:S(2)}) %collective-permute-start.8) | collective-permute-done | bytes 655392 | tf_op jit(solution)/shard_map/cond/branch_1_fun/ppermute | solution.py:26
  193.7 2.7 collective-permute-start.12
  196.4 14.9 %collective-permute-done.9 = bf16[160,2048]{1,0:T(8,128)(2,1)} collective-permute-done((bf16[160,2048]{1,0:T(8,128)(2,1)S(1)}, bf16[160,2048]{1,0:T(8,128)(2,1)}, u32[]{:S(2)}, u32[]{:S(2)}) %collective-permute-start.9) | collective-permute-done | bytes 655392 | tf_op jit(solution)/shard_map/cond/branch_1_fun/ppermute | solution.py:26
  211.4 2.7 collective-permute-start.13
  214.1 14.5 %collective-permute-done.10 = bf16[160,2048]{1,0:T(8,128)(2,1)} collective-permute-done((bf16[160,2048]{1,0:T(8,128)(2,1)}, bf16[160,2048]{1,0:T(8,128)(2,1)}, u32[]{:S(2)}, u32[]{:S(2)}) %collective-permute-start.10) | collective-permute-done | bytes 655392 | tf_op jit(solution)/shard_map/cond/branch_1_fun/ppermute | solution.py:26
  228.6 2.0 bitcast_dynamic-update-slice_fusion.15
  230.6 2.0 bitcast_dynamic-update-slice_fusion.14
  232.6 0.9 bitcast_dynamic-update-slice_fusion.13
  236.2 2.0 bitcast_dynamic-update-slice_fusion.9
  238.1 0.9 bitcast_dynamic-update-slice_fusion.8
  239.1 5.7 %gather_fusion.1 = bf16[8,160,2048]{2,1,0:T(8,128)(2,1)} fusion(bf16[8,160,2048]{2,1,0:T(8,128)(2,1)} %bitcast_dynamic-update-slice_fusion.8, s32[1024]{0:T(1024)S(1)} %pad_clamp_fusion.1), kind=kCustom, calls=%fused_computation.1 | custom fusion | bytes 10485792 | tf_op jit(solution)/shard_map/cond/branch_1_fun/gather | solution.py:31
  244.8 16.9 %convolution_convert_fusion.2 = bf16[1280,2048]{1,0:T(8,128)(2,1)} fusion(bf16[1,1024,2048]{2,1,0:T(8,128)(2,1)} %get-tuple-element.45, bf16[1280,2048]{1,0:T(8,128)(2,1)} %bitcast.96, bf16[1,2048,1024]{2,1,0:T(8,128)(2,1)} %get-tuple-element.44), kind=kOutput, calls=%fused_computation.30 | convolution fusion | flops 10742661120 | bytes 18874368 | tf_op jit(solution)/shard_map/cond/branch_1_fun/dot_general | solution.py:93
  263.4 69.5 %reduce-scatter.5.cloned.1.call-done = bf16[160,2048]{1,0:T(8,128)(2,1)} async-done(((bf16[1280,2048]{1,0:T(8,128)(2,1)}), bf16[160,2048]{1,0:T(8,128)(2,1)}) %reduce-scatter.5.cloned.1.call-update) | async-done | bytes 655376 | tf_op jit(solution)/shard_map/cond/branch_1_fun/reduce_scatter | solution.py:94
  332.9 1.6 fusion.15
  334.5 24.3 %all_to_all.10 = bf16[32,8,2048]{2,1,0:T(8,128)(2,1)S(1)} all-to-all(bf16[32,8,2048]{2,1,0:T(8,128)(2,1)S(1)} %bitcast.97), channel_id=1, replica_groups=mesh['dp'=8,'expert_0'=4,'expert_1'=4,'expert_2'=2] {'expert_0','expert_..., dimensions={0} | all-to-all | bytes 2097152 | tf_op jit(solution)/shard_map/all_to_all | solution.py:109
  358.8 1.5 fusion.22
  (54 shorter events, 6.9 us)
Async XLA Ops:
  6.5 2.0 copy-start
  10.0 155.2 %all-to-all-start = ((bf16[32,8,2048]{2,1,0:T(8,128)(2,1)}), bf16[32,8,2048]{2,1,0:T(8,128)(2,1)S(1)}, u32[]{:S(2)}, u32[]{:S(2)}) async-start(bf16[32,8,2048]{2,1,0:T(8,128)(2,1)} %fusion.23), calls=%async_computation.2 | async-start | bytes 2097152 | tf_op jit(solution)/shard_map/all_to_all | solution.py:55
  165.4 167.5 %reduce-scatter.5.cloned.1.call-start = ((), (), s32[]{:S(2)}) async-start(), calls=%async_computation.5 | async-start | bytes 5898240 | tf_op jit(solution)/shard_map/cond/branch_1_fun/reduce_scatter | solution.py:94
  166.0 10.8 %collective-permute-start.7 = (bf16[160,2048]{1,0:T(8,128)(2,1)S(1)}, bf16[160,2048]{1,0:T(8,128)(2,1)S(1)}, u32[]{:S(2)}, u32[]{:S(2)}) collective-permute-start(bf16[160,2048]{1,0:T(8,128)(2,1)S(1)} %convolution_convert_fusion.3), channel_id=1, source_target_pairs={{0,32},{32,64},{64,96},{96,128},{128,160},{160,192},{192,224},{224... | collective-permute-start | bytes 1966088 | tf_op jit(solution)/shard_map/cond/branch_1_fun/ppermute | solution.py:26
  176.8 16.9 %collective-permute-start.8 = (bf16[160,2048]{1,0:T(8,128)(2,1)S(1)}, bf16[160,2048]{1,0:T(8,128)(2,1)S(1)}, u32[]{:S(2)}, u32[]{:S(2)}) collective-permute-start(bf16[160,2048]{1,0:T(8,128)(2,1)S(1)} %collective-permute-done.7), channel_id=1, source_target_pairs={{0,32},{32,64},{64,96},{96,128},{128,160},{160,192},{192,224},{224... | collective-permute-start | bytes 1966088 | tf_op jit(solution)/shard_map/cond/branch_1_fun/ppermute | solution.py:26
  176.8 16.9 %collective-permute-start.11 = (bf16[160,2048]{1,0:T(8,128)(2,1)S(1)}, bf16[160,2048]{1,0:T(8,128)(2,1)S(1)}, u32[]{:S(2)}, u32[]{:S(2)}) collective-permute-start(bf16[160,2048]{1,0:T(8,128)(2,1)S(1)} %convolution_convert_fusion.3), channel_id=1, source_target_pairs={{32,0},{64,32},{96,64},{128,96},{160,128},{192,160},{224,192},{0,2... | collective-permute-start | bytes 1966088 | tf_op jit(solution)/shard_map/cond/branch_1_fun/ppermute | solution.py:28
  193.7 17.6 %collective-permute-start.9 = (bf16[160,2048]{1,0:T(8,128)(2,1)S(1)}, bf16[160,2048]{1,0:T(8,128)(2,1)}, u32[]{:S(2)}, u32[]{:S(2)}) collective-permute-start(bf16[160,2048]{1,0:T(8,128)(2,1)S(1)} %collective-permute-done.8), channel_id=1, source_target_pairs={{0,32},{32,64},{64,96},{96,128},{128,160},{160,192},{192,224},{224... | collective-permute-start | bytes 1966088 | tf_op jit(solution)/shard_map/cond/branch_1_fun/ppermute | solution.py:26
  193.7 17.6 %collective-permute-start.12 = (bf16[160,2048]{1,0:T(8,128)(2,1)S(1)}, bf16[160,2048]{1,0:T(8,128)(2,1)}, u32[]{:S(2)}, u32[]{:S(2)}) collective-permute-start(bf16[160,2048]{1,0:T(8,128)(2,1)S(1)} %collective-permute-done.11), channel_id=1, source_target_pairs={{32,0},{64,32},{96,64},{128,96},{160,128},{192,160},{224,192},{0,2... | collective-permute-start | bytes 1966088 | tf_op jit(solution)/shard_map/cond/branch_1_fun/ppermute | solution.py:28
  211.3 17.3 %collective-permute-start.10 = (bf16[160,2048]{1,0:T(8,128)(2,1)}, bf16[160,2048]{1,0:T(8,128)(2,1)}, u32[]{:S(2)}, u32[]{:S(2)}) collective-permute-start(bf16[160,2048]{1,0:T(8,128)(2,1)} %collective-permute-done.9), channel_id=1, source_target_pairs={{0,32},{32,64},{64,96},{96,128},{128,160},{160,192},{192,224},{224... | collective-permute-start | bytes 1966088 | tf_op jit(solution)/shard_map/cond/branch_1_fun/ppermute | solution.py:26
  211.4 26.8 %collective-permute-start.13 = (bf16[160,2048]{1,0:T(8,128)(2,1)}, bf16[160,2048]{1,0:T(8,128)(2,1)S(1)}, u32[]{:S(2)}, u32[]{:S(2)}) collective-permute-start(bf16[160,2048]{1,0:T(8,128)(2,1)} %collective-permute-done.12), channel_id=1, source_target_pairs={{32,0},{64,32},{96,64},{128,96},{160,128},{192,160},{224,192},{0,2... | collective-permute-start | bytes 1966088 | tf_op jit(solution)/shard_map/cond/branch_1_fun/ppermute | solution.py:28
  358.8 1.5 copy-start.1
Sparse Core Ops, SparseCore 0:
  261.8 71.0 reduce-scatter.4
